TPU v7x, 32 devices: a whole 2x2x4 slice. The times are simulated.
32 devices in a mesh: grp: 4 (over y, core), dev: 8 (over z, x).
Axes of the slice: x: 2, y: 2, z: 4, core: 2. Of those that a mesh axis runs over, the one named last changes fastest.
Arguments:
- basis_values: bfloat16 [128, 256, 512], P(('grp', 'dev')), may hold values from -1 to 1
- stored_density_blocks: bfloat16 [64, 128, 128], P('dev'), may hold values from -0.5 to 0.5
- device_request: int32 [32, 8, 8], P(('grp', 'dev')), may hold values from -1 to 7, as said below
- batch_blocks: int32 [128, 16], P(('grp', 'dev')), may hold values from 0 to 63, as said below
- batch_atom: int32 [128], P(('grp', 'dev')), may hold values from 0 to 999
- point_offset: float32 [3, 128, 256], P(None, ('grp', 'dev')), may hold values from -8 to 8
- point_weight: float32 [128, 256], P(('grp', 'dev')), may hold values from 0.02 to 0.5
- exchange_kernel: float32 [128, 256], P(('grp', 'dev')), may hold values from -3 to -0.3
- atom_xyz: float32 [3, 1000], replicated, may hold values from -15 to 15
Outputs:
- response_hamiltonian: bfloat16 [64, 128, 128], P('dev')
- response_density: float32 [128, 256], P(('grp', 'dev'))
- multipoles: float32 [4, 1000], replicated
Inputs may be any that keep to these rules, and one draw needn't show every extreme that they name: `device_request`: row d belongs to device d of grp+dev in grp-major order. Each row has exactly 32 entries other than -1, distinct for one owner; in every group one owner is asked for 8 blocks by every device of the group. `batch_blocks`: every entry points to an entry of its device's request row that is not -1.
All inputs are finite; a program needn't handle non-finite values.
Results may differ from a plain program's by a relative error of at most 0.004.
Values may be sent and summed in bfloat16 or wider, within the bound.
A program may use at most 64 MiB of HBM per device.

v0:
```python
import functools

import jax
import jax.numpy as jnp
from jax import lax
from jax.experimental import pallas as pl
from jax.experimental.pallas import tpu as pltpu
from jax.sharding import PartitionSpec as P

MESH = pl.DeviceIdType.MESH
LANES = 128
VMEM = pl.BlockSpec(memory_space=pltpu.VMEM)
SMEM = pl.BlockSpec(memory_space=pltpu.SMEM)
ANY = pl.BlockSpec(memory_space=pl.ANY)
F32 = jnp.float32
BF16 = jnp.bfloat16


def remote(src, dst, send, recv, grp, dev):
    return pltpu.make_async_remote_copy(
        src_ref=src,
        dst_ref=dst,
        send_sem=send,
        recv_sem=recv,
        device_id=(grp, dev),
        device_id_type=MESH,
    )


def meet(peers):
    barrier = pltpu.get_barrier_semaphore()
    for grp, dev in peers:
        pl.semaphore_signal(barrier, inc=1, device_id=(grp, dev), device_id_type=MESH)
    pl.semaphore_wait(barrier, len(peers))


def slot_of(request, blocks, b, p, capacity, own):
    position = blocks[b, p]
    owner = position // capacity
    return owner * own + request[0, owner, position - owner * capacity]


def flip(index, mask):
    out = index
    bit = 1
    while bit <= mask:
        if mask & bit:
            out = out + bit - 2 * bit * lax.rem(index // bit, 2)
        bit *= 2
    return out


def density_kernel(
    groups,
    devs,
    capacity,
    stored,
    request,
    blocks,
    batch_atom,
    offset,
    weight,
    xyz,
    values_any,
    density,
    own_rows,
    table_out,
    values,
    gathered,
    table,
    local_sem,
    send_a,
    recv_a,
    send_y,
    recv_y,
    send_b,
    recv_b,
    send_c,
    recv_c,
    send_d,
    recv_d,
):
    g, me = lax.axis_index("grp"), lax.axis_index("dev")
    own, tile = stored.shape[0], stored.shape[1]
    batches, points, width = values.shape
    rel = width // tile
    atoms = xyz.shape[1]
    half, quarter = own // 2, own // 4
    first_row = lax.rem(g, 2) * half
    lane_row = first_row + lax.rem(g // 2, 2) * quarter

    load = pltpu.make_async_copy(values_any, values, local_sem.at[0])
    load.start()
    mine = pltpu.make_async_copy(
        stored, gathered.at[pl.ds(me * own, own)], local_sem.at[1]
    )
    mine.start()
    peers = [(g, lax.rem(me + k, devs)) for k in range(1, devs)]
    peers += [(lax.rem(g + j, groups), me) for j in range(1, groups)]
    meet(peers)

    def piece(k):
        return pl.ds(flip(me, k) * own + lane_row, quarter)

    def source(k):
        return stored.at[pl.ds(lane_row, quarter)] if k == 0 else gathered.at[piece(k)]

    came = {}

    def onward(k):
        came[k + 1] = remote(
            source(k),
            gathered.at[piece(k)],
            send_a.at[k + 1],
            recv_a.at[k + 1],
            g,
            flip(me, 1),
        )
        came[k + 1].start()

    onward(0)
    for k in range(2, devs, 2):
        came[k] = remote(
            source(0), gathered.at[piece(0)], send_a.at[k], recv_a.at[k], g, flip(me, k)
        )
        came[k].start()

    centres = []
    spot = lax.broadcasted_iota(jnp.int32, (3, atoms), 1)
    for b in range(batches):
        centres.append(
            jnp.sum(jnp.where(spot == batch_atom[b], xyz[...], 0.0), axis=1, keepdims=True)
        )

    order = []
    for k in range(2, devs, 2):
        order += [k, k - 1]
    order.append(devs - 1)
    sideways, passed = {}, []

    def hand_over(k):
        sideways[k].wait_recv()
        rows = pl.ds(flip(me, k) * own + first_row, half)
        copy = remote(
            gathered.at[rows], gathered.at[rows], send_b.at[k], recv_b.at[k], flip(g, 1), me
        )
        copy.start()
        passed.append(copy)

    for step, k in enumerate(order):
        came[k].wait_recv()
        sideways[k] = remote(
            gathered.at[piece(k)],
            gathered.at[piece(k)],
            send_y.at[k],
            recv_y.at[k],
            flip(g, 2),
            me,
        )
        sideways[k].start()
        if k % 2 == 0:
            onward(k)
        if step >= 2:
            hand_over(order[step - 2])
    for k in order[-2:]:
        hand_over(k)
    out = list(came.values()) + list(sideways.values())
    load.wait()
    mine.wait()
    for copy in passed:
        copy.wait_recv()

    lane = lax.broadcasted_iota(jnp.int32, (1, LANES), 1)
    for b in range(batches):
        matrix = jnp.concatenate(
            [
                jnp.concatenate(
                    [
                        gathered[slot_of(request, blocks, b, i * rel + j, capacity, own)]
                        for j in range(rel)
                    ],
                    axis=1,
                )
                for i in range(rel)
            ],
            axis=0,
        )
        left = jnp.dot(values[b], matrix, preferred_element_type=F32)
        product = left * values[b].astype(F32)
        folded = product[:, :tile]
        for i in range(1, rel):
            folded = folded + product[:, i * tile : (i + 1) * tile]
        row = jnp.sum(folded.T, axis=0, keepdims=True)
        density[pl.ds(b, 1), :] = row
        weighted = row * weight[pl.ds(b, 1), :]
        parts = [jnp.sum(weighted, axis=1, keepdims=True)]
        for k in range(3):
            parts.append(
                jnp.sum(weighted * offset[k, pl.ds(b, 1), :], axis=1, keepdims=True)
            )
        parts += [centres[b][k : k + 1] for k in range(3)]
        entry = jnp.zeros((1, LANES), F32) + batch_atom[b].astype(F32)
        for k, part in enumerate(parts):
            entry = jnp.where(lane == k, part, entry)
        own_rows[pl.ds(b, 1), :] = entry
        table[me, g, pl.ds(b, 1), :] = entry

    first = []
    for j in range(1, groups):
        copy = remote(
            table.at[me, g],
            table.at[me, g],
            send_c.at[j],
            recv_c.at[j],
            lax.rem(g + j, groups),
            me,
        )
        copy.start()
        first.append(copy)
    for copy in first:
        copy.wait_recv()
    second = []
    for k in range(1, devs):
        copy = remote(
            table.at[me], table.at[me], send_d.at[k], recv_d.at[k], g, lax.rem(me + k, devs)
        )
        copy.start()
        second.append(copy)
    for copy in out + passed + first:
        copy.wait_send()
    for copy in second:
        copy.wait_recv()
    for copy in second:
        copy.wait_send()
    for d in range(devs):
        table_out[d * groups : (d + 1) * groups] = table[d]


def term_kernel(
    capacity,
    own,
    request,
    blocks,
    values,
    table,
    own_rows,
    density,
    weight,
    exchange,
    offset,
    part,
    multipoles,
    density_out,
    total,
):
    batches, points, width = values.shape
    tile = part.shape[1]
    rel = width // tile
    devices = table.shape[0]
    atoms = multipoles.shape[1]
    chunk = min(devices, 32)
    total[...] = jnp.zeros_like(total)
    density_out[...] = density[...]

    places = [
        [own_rows[pl.ds(b, 1), 4 + k : 5 + k] + offset[k, pl.ds(b, 1), :] for k in range(3)]
        for b in range(batches)
    ]
    spot = lax.broadcasted_iota(jnp.int32, (1, atoms), 1).astype(F32)

    def gather(step, carry):
        fields, moments = carry
        fields, moments = list(fields), list(moments)
        for source in range(batches):
            rows = table[pl.ds(step * chunk, chunk), source, :]
            column = [rows[:, k : k + 1] for k in range(8)]
            hit = column[7] == spot
            for k in range(4):
                moments[k] = moments[k] + jnp.sum(
                    jnp.where(hit, column[k], 0.0), axis=0, keepdims=True
                )
            for b in range(batches):
                gap = [places[b][k] - column[4 + k] for k in range(3)]
                inverse = lax.rsqrt(
                    gap[0] * gap[0] + gap[1] * gap[1] + gap[2] * gap[2] + 1.0
                )
                cube = inverse * inverse * inverse
                dipole = column[1] * gap[0] + column[2] * gap[1] + column[3] * gap[2]
                fields[b] = fields[b] + jnp.sum(
                    column[0] * inverse + dipole * cube, axis=0, keepdims=True
                )
        return tuple(fields), tuple(moments)

    carry = (
        tuple(jnp.zeros((1, points), F32) for _ in range(batches)),
        tuple(jnp.zeros((1, atoms), F32) for _ in range(4)),
    )
    if devices == chunk:
        fields, moments = gather(0, carry)
    else:
        fields, moments = lax.fori_loop(0, devices // chunk, gather, carry)
    for k in range(4):
        multipoles[pl.ds(k, 1), :] = moments[k]

    for b in range(batches):
        pick = pl.ds(b, 1)
        factors = (
            weight[pick, :] * exchange[pick, :] * density[pick, :],
            weight[pick, :] * fields[b],
        )
        wide = values[b].astype(F32)
        scaled = []
        for factor in factors:
            column = jnp.broadcast_to(factor, (tile, points)).T
            scaled.append(
                jnp.concatenate(
                    [
                        (wide[:, i * tile : (i + 1) * tile] * column).astype(BF16)
                        for i in range(rel)
                    ],
                    axis=1,
                )
            )
        stacked = jnp.concatenate(scaled, axis=0)
        doubled = jnp.concatenate([values[b], values[b]], axis=0)
        term = lax.dot_general(
            stacked, doubled, (((0,), (0,)), ((), ())), preferred_element_type=F32
        )
        for i in range(rel):
            for j in range(rel):
                slot = slot_of(request, blocks, b, i * rel + j, capacity, own)
                total[slot] += term[i * tile : (i + 1) * tile, j * tile : (j + 1) * tile]
    part[...] = total[...].astype(BF16)


def reduce_kernel(
    groups,
    devs,
    part,
    result,
    paired,
    sent_1,
    came_1,
    sent_2,
    came_2,
    outgoing,
    arrived,
    across,
    final,
    send_a,
    recv_a,
    send_1,
    recv_1,
    send_2,
    recv_2,
    send_b,
    recv_b,
    send_c,
    recv_c,
    send_d,
    recv_d,
):
    g, me = lax.axis_index("grp"), lax.axis_index("dev")
    own = result.shape[0]
    half, quarter = own // 2, own // 4
    quads = groups // 4
    quad, lane = g // 4, lax.rem(g, 4)
    core, side = lax.rem(g, 2), lax.rem(g // 2, 2)
    pair, beside = flip(g, 1), flip(g, 2)
    turn_y, turn_x = 1 - 2 * side, 1 - 2 * lax.rem(me, 2)
    one = (g + (1 - core) * 2 * turn_y, me + core * turn_x)
    two = (g + core * 2 * turn_y, me + (1 - core) * turn_x)

    peers = [(pair, me), (beside, me)]
    peers += [(g, flip(me, k)) for k in [1, *range(2, devs, 2)]]
    peers += [(lax.rem(quad + j, quads) * 4 + lane, me) for j in range(1, quads)]
    meet(peers)

    order = list(range(devs - 1, -1, -1))
    halves, first, second, out = {}, {}, {}, {}
    for k in order:
        halves[k] = remote(
            part.at[pl.ds(flip(me, k) * own + (1 - core) * half, half)],
            paired.at[k],
            send_a.at[k],
            recv_a.at[k],
            pair,
            me,
        )
        halves[k].start()

    def of_pair(a, b, k):
        over_x = core * a + (1 - core) * b
        which = side + ((1 - core) * a + core * b) * turn_y
        row = (flip(me, k) + over_x * turn_x) * own + core * half + which * quarter
        here = part[pl.ds(row, quarter)]
        there = paired[k + over_x, pl.ds(which * quarter, quarter)]
        return here.astype(F32) + there.astype(F32)

    def of_four(b, k):
        first[k + b].wait_recv()
        return of_pair(0, b, k) + came_1[k + b].astype(F32)

    def of_eight(k):
        second[k].wait_recv()
        return of_four(0, k) + came_2[k // 2].astype(F32)

    def step_1(k):
        halves[k + 1].wait_recv()
        halves[k].wait_recv()
        for b in (1, 0):
            slot = k + b
            sent_1[slot] = of_pair(1, b, k).astype(BF16)
            first[slot] = remote(
                sent_1.at[slot], came_1.at[slot], send_1.at[slot], recv_1.at[slot], *one
            )
            first[slot].start()

    def step_2(k):
        slot = k // 2
        sent_2[slot] = of_four(1, k).astype(BF16)
        second[k] = remote(
            sent_2.at[slot], came_2.at[slot], send_2.at[slot], recv_2.at[slot], *two
        )
        second[k].start()

    def step_3(k):
        slot = k // 2
        outgoing[slot] = of_eight(k).astype(BF16)
        out[k] = remote(
            outgoing.at[slot],
            arrived.at[slot],
            send_b.at[slot],
            recv_b.at[slot],
            g,
            flip(me, k),
        )
        out[k].start()

    planes = list(range(devs - 2, -1, -2))
    for step, k in enumerate(planes):
        step_1(k)
        if step >= 1:
            step_2(planes[step - 1])
        if step >= 2:
            step_3(planes[step - 2])
    step_2(0)
    for k in planes[-2:-1]:
        step_3(k)
    whole = of_eight(0)
    for k in planes[:-1]:
        out[k].wait_recv()
        whole = whole + arrived[k // 2].astype(F32)
    others = []
    if quads > 1:
        across[quad] = whole.astype(BF16)
        for j in range(1, quads):
            copy = remote(
                across.at[quad],
                across.at[quad],
                send_c.at[j],
                recv_c.at[j],
                lax.rem(quad + j, quads) * 4 + lane,
                me,
            )
            copy.start()
            others.append(copy)
        for copy in others:
            copy.wait_recv()
        whole = across[0].astype(F32)
        for j in range(1, quads):
            whole = whole + across[j].astype(F32)
    part_rows = pl.ds(core * half + side * quarter, quarter)
    half_rows = pl.ds(core * half, half)
    final[part_rows] = whole.astype(BF16)
    for step, (where, to) in enumerate(((part_rows, beside), (half_rows, pair))):
        copy = remote(
            final.at[where], final.at[where], send_d.at[step], recv_d.at[step], to, me
        )
        copy.start()
        copy.wait_recv()
        others.append(copy)
    for copy in [*halves.values(), *first.values(), *second.values(), *out.values(), *others]:
        copy.wait_send()
    result[...] = final[...]


def on_device(
    groups,
    devs,
    basis_values,
    stored_density_blocks,
    device_request,
    batch_blocks,
    batch_atom,
    point_offset,
    point_weight,
    exchange_kernel,
    atom_xyz,
):
    batches, points, width = basis_values.shape
    own, tile = stored_density_blocks.shape[:2]
    capacity = device_request.shape[2]
    slots = devs * own
    atoms = atom_xyz.shape[1]
    half, quarter = own // 2, own // 4
    request = device_request
    dma = pltpu.SemaphoreType.DMA

    density, own_rows, table = pl.pallas_call(
        functools.partial(density_kernel, groups, devs, capacity),
        out_shape=(
            jax.ShapeDtypeStruct((batches, points), F32),
            jax.ShapeDtypeStruct((batches, LANES), F32),
            jax.ShapeDtypeStruct((devs * groups, batches, LANES), F32),
        ),
        in_specs=[VMEM, SMEM, SMEM, SMEM, VMEM, VMEM, VMEM, ANY],
        out_specs=(VMEM, VMEM, VMEM),
        scratch_shapes=[
            pltpu.VMEM((batches, points, width), BF16),
            pltpu.VMEM((slots, tile, tile), BF16),
            pltpu.VMEM((devs, groups, batches, LANES), F32),
            dma((2,)),
            dma((devs,)),
            dma((devs,)),
            dma((devs,)),
            dma((devs,)),
            dma((devs,)),
            dma((devs,)),
            dma((groups,)),
            dma((groups,)),
            dma((devs,)),
            dma((devs,)),
        ],
        compiler_params=pltpu.CompilerParams(collective_id=0, has_side_effects=True),
    )(
        stored_density_blocks,
        request,
        batch_blocks,
        batch_atom,
        point_offset,
        point_weight,
        atom_xyz,
        basis_values,
    )

    part, multipoles, density = pl.pallas_call(
        functools.partial(term_kernel, capacity, own),
        out_shape=(
            jax.ShapeDtypeStruct((slots, tile, tile), BF16),
            jax.ShapeDtypeStruct((4, atoms), F32),
            jax.ShapeDtypeStruct((batches, points), F32),
        ),
        in_specs=[SMEM, SMEM, VMEM, VMEM, VMEM, VMEM, VMEM, VMEM, VMEM],
        out_specs=(VMEM, VMEM, VMEM),
        scratch_shapes=[pltpu.VMEM((slots, tile, tile), F32)],
    )(
        request,
        batch_blocks,
        basis_values,
        table,
        own_rows,
        density,
        point_weight,
        exchange_kernel,
        point_offset,
    )

    hamiltonian = pl.pallas_call(
        functools.partial(reduce_kernel, groups, devs),
        out_shape=jax.ShapeDtypeStruct((own, tile, tile), BF16),
        in_specs=[VMEM],
        out_specs=VMEM,
        scratch_shapes=[
            pltpu.VMEM((devs, half, tile, tile), BF16),
            pltpu.VMEM((devs, quarter, tile, tile), BF16),
            pltpu.VMEM((devs, quarter, tile, tile), BF16),
            pltpu.VMEM((devs // 2, quarter, tile, tile), BF16),
            pltpu.VMEM((devs // 2, quarter, tile, tile), BF16),
            pltpu.VMEM((devs // 2, quarter, tile, tile), BF16),
            pltpu.VMEM((devs // 2, quarter, tile, tile), BF16),
            pltpu.VMEM((groups // 4, quarter, tile, tile), BF16),
            pltpu.VMEM((own, tile, tile), BF16),
            dma((devs,)),
            dma((devs,)),
            dma((devs,)),
            dma((devs,)),
            dma((devs,)),
            dma((devs,)),
            dma((devs,)),
            dma((devs,)),
            dma((groups // 4,)),
            dma((groups // 4,)),
            dma((2,)),
            dma((2,)),
        ],
        compiler_params=pltpu.CompilerParams(collective_id=1, has_side_effects=True),
    )(part)
    return (hamiltonian, density, multipoles)


def solution(mesh):
    return jax.shard_map(
        functools.partial(on_device, mesh.shape["grp"], mesh.shape["dev"]),
        mesh=mesh,
        in_specs=(
            P(("grp", "dev"), None, None),
            P("dev", None, None),
            P(("grp", "dev"), None, None),
            P(("grp", "dev"), None),
            P(("grp", "dev")),
            P(None, ("grp", "dev"), None),
            P(("grp", "dev"), None),
            P(("grp", "dev"), None),
            P(),
        ),
        out_specs=(P("dev", None, None), P(("grp", "dev"), None), P()),
        check_vma=False,
    )
```

profile of v0, /device:TPU:0, one launch (start us, length us, event | category | flops | bytes accessed | tf_op | source)
XLA Modules:
  0.0 66.5 jit_solution(17183307516161124424)
XLA Ops:
  0.6 31.9 %shard_map.112 = (f32[4,256]{1,0:T(4,128)}, f32[4,128]{1,0:T(4,128)}, f32[32,4,128]{2,1,0:T(4,128)}) custom-call(bf16[8,128,128]{2,1,0:T(8,128)(2,1)} %stored.1, s32[1,8,8]{2,1,0:T(8,128)} %request.3, s32[4,16]{1,0:T(4,128)} %blocks.3, s32[4]{0:T(128)} %batch_atom.1, f32[3,4,256]{2,1,0:T(4,128)} %offset.3, f32[4,256]{1,0:T(4,128)} %weight.3, f32[3,1000]{1,0:T(4,128)} %xyz.1, ...), custom_call_target="tpu_custom_call" | custom-call | tf_op jit(solution)/shard_map/pallas_call | solution.py:510
  32.6 6.2 %shard_map.113 = (bf16[64,128,128]{2,1,0:T(8,128)(2,1)}, f32[4,1000]{1,0:T(4,128)}, f32[4,256]{1,0:T(4,128)}) custom-call(s32[1,8,8]{2,1,0:T(8,128)} %request.3, s32[4,16]{1,0:T(4,128)} %blocks.3, bf16[4,256,512]{2,1,0:T(8,128)(2,1)} %values.1, f32[32,4,128]{2,1,0:T(4,128)} %get-tuple-element.9.table, f32[4,128]{1,0:T(4,128)} %get-tuple-element.10.own_rows, ...), custom_call_target="tpu_custom_call" | custom-call | tf_op jit(solution)/shard_map/pallas_call | solution.py:547
  38.8 26.0 %shard_map.114 = bf16[8,128,128]{2,1,0:T(8,128)(2,1)} custom-call(bf16[64,128,128]{2,1,0:T(8,128)(2,1)} %get-tuple-element.12.part), custom_call_target="tpu_custom_call" | custom-call | tf_op jit(solution)/shard_map/pallas_call | solution.py:569
  64.8 1.7 %copy.13 = bf16[8,128,128]{2,1,0:T(8,128)(2,1)} copy(bf16[8,128,128]{2,1,0:T(8,128)(2,1)} %shard_map.114) | data formatting | bytes 524288
where the time goes:
time: 66.7 us; the launch traced here: 66.5 us
  Pallas kernels  64.2 us (96%)
  local copies, waits for them, and re-layouts  1.67 us (3%)
    pallas_call x1, Pallas kernels, on_device(): pl.pallas_call(functools.partial(density_kernel, groups, devs, capacity),...  31.9 us
    pallas_call x1, Pallas kernels, on_device(): pl.pallas_call(functools.partial(reduce_kernel, groups, devs), out_shape=...  26 us
    pallas_call x1, Pallas kernels, on_device(): pl.pallas_call(functools.partial(term_kernel, capacity, own), out_shape=(...  6.24 us
    unnamed x1, local copies, waits for them, and re-layouts  1.67 us

commit v1 on v0

v1 whole, which is shorter than its diff:
```python
import functools

import jax
import jax.numpy as jnp
from jax import lax
from jax.experimental import pallas as pl
from jax.experimental.pallas import tpu as pltpu
from jax.sharding import PartitionSpec as P

MESH = pl.DeviceIdType.MESH
LANES = 128
VMEM = pl.BlockSpec(memory_space=pltpu.VMEM)
SMEM = pl.BlockSpec(memory_space=pltpu.SMEM)
ANY = pl.BlockSpec(memory_space=pl.ANY)
F32 = jnp.float32
BF16 = jnp.bfloat16


def remote(src, dst, send, recv, grp, dev):
    return pltpu.make_async_remote_copy(
        src_ref=src,
        dst_ref=dst,
        send_sem=send,
        recv_sem=recv,
        device_id=(grp, dev),
        device_id_type=MESH,
    )


def meet(peers):
    barrier = pltpu.get_barrier_semaphore()
    for grp, dev in peers:
        pl.semaphore_signal(barrier, inc=1, device_id=(grp, dev), device_id_type=MESH)
    pl.semaphore_wait(barrier, len(peers))


def slot_of(request, blocks, b, p, capacity, own):
    position = blocks[b, p]
    owner = position // capacity
    return owner * own + request[0, owner, position - owner * capacity]


def flip(index, mask):
    out = index
    bit = 1
    while bit <= mask:
        if mask & bit:
            out = out + bit - 2 * bit * lax.rem(index // bit, 2)
        bit *= 2
    return out


def whole_kernel(
    groups,
    devs,
    request,
    blocks,
    batch_atom,
    stored_any,
    values_any,
    offset_any,
    weight_any,
    exchange_any,
    xyz_any,
    result,
    density,
    table,
    gathered,
    values,
    turned,
    offset,
    weight,
    exchange,
    xyz,
    sums,
    picks,
    part,
    paired,
    sent_1,
    came_1,
    sent_2,
    came_2,
    outgoing,
    arrived,
    across,
    final,
    local_sem,
    gather_sems,
    table_sems,
    wide_sems,
    pair_sems,
    end_sems,
):
    g, me = lax.axis_index("grp"), lax.axis_index("dev")
    own, tile = result.shape[0], result.shape[1]
    slots, capacity = gathered.shape[0], request.shape[2]
    batches, points, width = values.shape
    rel = width // tile
    pairs = batches * rel * rel
    atoms = xyz.shape[1]
    devices = groups * devs
    half, quarter = own // 2, own // 4
    send_a, recv_a, send_y, recv_y, send_b, recv_b = (gather_sems.at[i] for i in range(6))

    mine = pltpu.make_async_copy(
        stored_any, gathered.at[pl.ds(me * own, own)], local_sem.at[0]
    )
    mine.start()
    loads = []
    for i, (source, target) in enumerate(
        (
            (values_any, values),
            (xyz_any, xyz),
            (offset_any, offset),
            (weight_any, weight),
            (exchange_any, exchange),
        )
    ):
        loads.append(pltpu.make_async_copy(source, target, local_sem.at[1 + i]))
        loads[-1].start()
    others = [
        (lax.rem(g + j, groups), lax.rem(me + k, devs))
        for j in range(groups)
        for k in range(devs)
        if j or k
    ]
    meet(others)
    mine.wait()

    first_row = lax.rem(g, 2) * half
    lane_row = first_row + lax.rem(g // 2, 2) * quarter

    def piece(k):
        return gathered.at[pl.ds(flip(me, k) * own + lane_row, quarter)]

    came = {}

    def onward(k):
        came[k + 1] = remote(
            piece(k), piece(k), send_a.at[k + 1], recv_a.at[k + 1], g, flip(me, 1)
        )
        came[k + 1].start()

    onward(0)
    for k in range(2, devs, 2):
        came[k] = remote(piece(0), piece(0), send_a.at[k], recv_a.at[k], g, flip(me, k))
        came[k].start()

    for copy in loads:
        copy.wait()
    lane = lax.broadcasted_iota(jnp.int32, (1, LANES), 1)
    slot_of_pair = [
        slot_of(request, blocks, p // (rel * rel), p % (rel * rel), capacity, own)
        for p in range(pairs)
    ]
    known = jnp.full((1, LANES), -1, jnp.int32)
    for p in range(pairs):
        known = jnp.where(lane == p, slot_of_pair[p], known)
    for p in range(pairs):
        same = known == slot_of_pair[p]
        before = jnp.max(jnp.where(same & (lane < p), lane, -1))
        last = jnp.max(jnp.where(same, lane, -1))
        picks[0, p] = jnp.where(before < 0, 2 * pairs, before)
        picks[1, p] = jnp.where(before < 0, last, before + pairs)
    for s in range(slots):
        last = jnp.max(jnp.where(known == s, lane, -1))
        picks[2, s] = jnp.where(last < 0, 2 * pairs, last + pairs)
    for b in range(batches):
        turned[b] = values[b].T
    sums[2 * pairs] = jnp.zeros((tile, tile), F32)
    spot = lax.broadcasted_iota(jnp.int32, (3, atoms), 1)
    centres = [
        jnp.sum(jnp.where(spot == batch_atom[b], xyz[...], 0.0), axis=1, keepdims=True)
        for b in range(batches)
    ]
    entry = jnp.zeros((1, LANES), F32)
    for b in range(batches):
        for k in range(3):
            entry = jnp.where(lane == b * 8 + 4 + k, centres[b][k : k + 1], entry)
        entry = jnp.where(lane == b * 8 + 7, batch_atom[b].astype(F32), entry)

    order = []
    for k in range(2, devs, 2):
        order += [k, k - 1]
    order.append(devs - 1)
    sideways, passed = {}, []

    def hand_over(k):
        sideways[k].wait_recv()
        rows = pl.ds(flip(me, k) * own + first_row, half)
        copy = remote(
            gathered.at[rows], gathered.at[rows], send_b.at[k], recv_b.at[k], flip(g, 1), me
        )
        copy.start()
        passed.append(copy)

    for step, k in enumerate(order):
        came[k].wait_recv()
        sideways[k] = remote(piece(k), piece(k), send_y.at[k], recv_y.at[k], flip(g, 2), me)
        sideways[k].start()
        if k % 2 == 0:
            onward(k)
        if step >= 2:
            hand_over(order[step - 2])
    for k in order[-2:]:
        hand_over(k)
    pending = list(came.values()) + list(sideways.values()) + passed
    for copy in passed:
        copy.wait_recv()

    for b in range(batches):
        tiles = [
            [
                gathered[slot_of(request, blocks, b, i * rel + j, capacity, own)]
                for j in range(rel)
            ]
            for i in range(rel)
        ]
        matrix = jnp.concatenate([jnp.concatenate(row, axis=1) for row in tiles], axis=0)
        right = jnp.dot(matrix, turned[b], preferred_element_type=F32)
        row = jnp.sum(right * turned[b].astype(F32), axis=0, keepdims=True)
        density[pl.ds(b, 1), :] = row
        weighted = row * weight[pl.ds(b, 1), :]
        moments = [jnp.sum(weighted, axis=1, keepdims=True)]
        for k in range(3):
            moments.append(
                jnp.sum(weighted * offset[k, pl.ds(b, 1), :], axis=1, keepdims=True)
            )
        for k in range(4):
            entry = jnp.where(lane == b * 8 + k, moments[k], entry)
    here = g * devs + me
    table[here] = entry

    spread = []
    for i, (to_g, to_me) in enumerate(others[::-1]):
        copy = remote(
            table.at[here], table.at[here], table_sems.at[0, i], table_sems.at[1, i], to_g, to_me
        )
        copy.start()
        spread.append(copy)

    def accumulate(b, factor, index, base):
        scaled = (turned[b].astype(F32) * factor).astype(BF16)
        term = jnp.dot(scaled, values[b], preferred_element_type=F32)
        for i in range(rel):
            for j in range(rel):
                p = (b * rel + i) * rel + j
                sums[base + p] = (
                    term[i * tile : (i + 1) * tile, j * tile : (j + 1) * tile]
                    + sums[picks[index, p]]
                )

    for b in range(batches):
        pick = pl.ds(b, 1)
        accumulate(b, weight[pick, :] * exchange[pick, :] * density[pick, :], 0, 0)
    places = [
        [centres[b][k : k + 1] + offset[k, pl.ds(b, 1), :] for k in range(3)]
        for b in range(batches)
    ]
    for copy in spread:
        copy.wait_recv()

    chunk = min(devices, 32)

    def gather(step, fields):
        fields = list(fields)
        rows = table[pl.ds(step * chunk, chunk), 0, :]
        for source in range(batches):
            column = [rows[:, source * 8 + k : source * 8 + k + 1] for k in range(7)]
            for b in range(batches):
                gap = [places[b][k] - column[4 + k] for k in range(3)]
                inverse = lax.rsqrt(
                    gap[0] * gap[0] + gap[1] * gap[1] + gap[2] * gap[2] + 1.0
                )
                cube = inverse * inverse * inverse
                dipole = column[1] * gap[0] + column[2] * gap[1] + column[3] * gap[2]
                fields[b] = fields[b] + jnp.sum(
                    column[0] * inverse + dipole * cube, axis=0, keepdims=True
                )
        return tuple(fields)

    fields = tuple(jnp.zeros((1, points), F32) for _ in range(batches))
    if devices == chunk:
        fields = gather(0, fields)
    else:
        fields = lax.fori_loop(0, devices // chunk, gather, fields)
    for b in range(batches):
        accumulate(b, weight[pl.ds(b, 1), :] * fields[b], 1, pairs)
    for copy in pending + spread:
        copy.wait_send()

    quads = groups // 4
    quad, corner = g // 4, lax.rem(g, 4)
    core, side = lax.rem(g, 2), lax.rem(g // 2, 2)
    pair, beside = flip(g, 1), flip(g, 2)
    turn_y, turn_x = 1 - 2 * side, 1 - 2 * lax.rem(me, 2)
    one = (g + (1 - core) * 2 * turn_y, me + core * turn_x)
    two = (g + core * 2 * turn_y, me + (1 - core) * turn_x)

    send_a, recv_a, send_1, recv_1, send_2, recv_2, send_b, recv_b = (
        wide_sems.at[i] for i in range(8)
    )
    send_c, recv_c = pair_sems.at[0], pair_sems.at[1]
    send_d, recv_d = end_sems.at[0], end_sems.at[1]

    def fill(owner, row, count):
        for r in range(count):
            s = owner * own + row + r
            part[s] = sums[picks[2, s]].astype(BF16)

    order = list(range(devs - 1, -1, -1))
    halves, first, second, out = {}, {}, {}, {}
    for k in order:
        fill(flip(me, k), (1 - core) * half, half)
        halves[k] = remote(
            part.at[pl.ds(flip(me, k) * own + (1 - core) * half, half)],
            paired.at[k],
            send_a.at[k],
            recv_a.at[k],
            pair,
            me,
        )
        halves[k].start()

    for k in order:
        fill(flip(me, k), core * half, half)

    def of_pair(a, b, k):
        over_x = core * a + (1 - core) * b
        which = side + ((1 - core) * a + core * b) * turn_y
        row = (flip(me, k) + over_x * turn_x) * own + core * half + which * quarter
        here = part[pl.ds(row, quarter)]
        there = paired[k + over_x, pl.ds(which * quarter, quarter)]
        return here.astype(F32) + there.astype(F32)

    def of_four(b, k):
        first[k + b].wait_recv()
        return of_pair(0, b, k) + came_1[k + b].astype(F32)

    def of_eight(k):
        second[k].wait_recv()
        return of_four(0, k) + came_2[k // 2].astype(F32)

    def step_1(k):
        halves[k + 1].wait_recv()
        halves[k].wait_recv()
        for b in (1, 0):
            slot = k + b
            sent_1[slot] = of_pair(1, b, k).astype(BF16)
            first[slot] = remote(
                sent_1.at[slot], came_1.at[slot], send_1.at[slot], recv_1.at[slot], *one
            )
            first[slot].start()

    def step_2(k):
        slot = k // 2
        sent_2[slot] = of_four(1, k).astype(BF16)
        second[k] = remote(
            sent_2.at[slot], came_2.at[slot], send_2.at[slot], recv_2.at[slot], *two
        )
        second[k].start()

    def step_3(k):
        slot = k // 2
        outgoing[slot] = of_eight(k).astype(BF16)
        out[k] = remote(
            outgoing.at[slot],
            arrived.at[slot],
            send_b.at[slot],
            recv_b.at[slot],
            g,
            flip(me, k),
        )
        out[k].start()

    planes = list(range(devs - 2, -1, -2))
    for step, k in enumerate(planes):
        step_1(k)
        if step >= 1:
            step_2(planes[step - 1])
        if step >= 2:
            step_3(planes[step - 2])
    step_2(0)
    for k in planes[-2:-1]:
        step_3(k)
    whole = of_eight(0)
    for k in planes[:-1]:
        out[k].wait_recv()
        whole = whole + arrived[k // 2].astype(F32)
    late = []
    if quads > 1:
        across[quad] = whole.astype(BF16)
        for j in range(1, quads):
            copy = remote(
                across.at[quad],
                across.at[quad],
                send_c.at[j],
                recv_c.at[j],
                lax.rem(quad + j, quads) * 4 + corner,
                me,
            )
            copy.start()
            late.append(copy)
        for copy in late:
            copy.wait_recv()
        whole = across[0].astype(F32)
        for j in range(1, quads):
            whole = whole + across[j].astype(F32)
    part_rows = pl.ds(core * half + side * quarter, quarter)
    half_rows = pl.ds(core * half, half)
    final[part_rows] = whole.astype(BF16)
    for step, (where, to) in enumerate(((part_rows, beside), (half_rows, pair))):
        copy = remote(
            final.at[where], final.at[where], send_d.at[step], recv_d.at[step], to, me
        )
        copy.start()
        copy.wait_recv()
        late.append(copy)
    for copy in [*halves.values(), *first.values(), *second.values(), *out.values(), *late]:
        copy.wait_send()
    result[...] = final[...]


def finish_kernel(batches, hamiltonian, density, table, result, density_out, multipoles):
    result[...] = hamiltonian[...]
    density_out[...] = density[...]
    devices, atoms = table.shape[0], multipoles.shape[1]
    chunk = min(devices, 32)
    spot = lax.broadcasted_iota(jnp.int32, (1, atoms), 1).astype(F32)

    def gather(step, moments):
        moments = list(moments)
        rows = table[pl.ds(step * chunk, chunk), 0, :]
        for source in range(batches):
            hit = rows[:, source * 8 + 7 : source * 8 + 8] == spot
            for k in range(4):
                column = rows[:, source * 8 + k : source * 8 + k + 1]
                moments[k] = moments[k] + jnp.sum(
                    jnp.where(hit, column, 0.0), axis=0, keepdims=True
                )
        return tuple(moments)

    moments = tuple(jnp.zeros((1, atoms), F32) for _ in range(4))
    if devices == chunk:
        moments = gather(0, moments)
    else:
        moments = lax.fori_loop(0, devices // chunk, gather, moments)
    for k in range(4):
        multipoles[pl.ds(k, 1), :] = moments[k]


def on_device(
    groups,
    devs,
    basis_values,
    stored_density_blocks,
    device_request,
    batch_blocks,
    batch_atom,
    point_offset,
    point_weight,
    exchange_kernel,
    atom_xyz,
):
    batches, points, width = basis_values.shape
    own, tile = stored_density_blocks.shape[:2]
    slots = devs * own
    atoms = atom_xyz.shape[1]
    devices = groups * devs
    half, quarter = own // 2, own // 4
    pairs = batches * (width // tile) ** 2
    dma = pltpu.SemaphoreType.DMA

    hamiltonian, density, table = pl.pallas_call(
        functools.partial(whole_kernel, groups, devs),
        out_shape=(
            pltpu.VMEM((own, tile, tile), BF16),
            pltpu.VMEM((batches, points), F32),
            pltpu.VMEM((devices, 1, LANES), F32),
        ),
        in_specs=[SMEM, SMEM, SMEM, ANY, ANY, ANY, ANY, ANY, ANY],
        out_specs=(VMEM, VMEM, VMEM),
        scratch_shapes=[
            pltpu.VMEM((slots, tile, tile), BF16),
            pltpu.VMEM((batches, points, width), BF16),
            pltpu.VMEM((batches, width, points), BF16),
            pltpu.VMEM(point_offset.shape, F32),
            pltpu.VMEM((batches, points), F32),
            pltpu.VMEM((batches, points), F32),
            pltpu.VMEM(atom_xyz.shape, F32),
            pltpu.VMEM((2 * pairs + 1, tile, tile), F32),
            pltpu.SMEM((3, max(slots, pairs)), jnp.int32),
            pltpu.VMEM((slots, tile, tile), BF16),
            pltpu.VMEM((devs, half, tile, tile), BF16),
            pltpu.VMEM((devs, quarter, tile, tile), BF16),
            pltpu.VMEM((devs, quarter, tile, tile), BF16),
            pltpu.VMEM((devs // 2, quarter, tile, tile), BF16),
            pltpu.VMEM((devs // 2, quarter, tile, tile), BF16),
            pltpu.VMEM((devs // 2, quarter, tile, tile), BF16),
            pltpu.VMEM((devs // 2, quarter, tile, tile), BF16),
            pltpu.VMEM((groups // 4, quarter, tile, tile), BF16),
            pltpu.VMEM((own, tile, tile), BF16),
            dma((6,)),
            dma((6, devs)),
            dma((2, devices)),
            dma((8, devs)),
            dma((2, groups // 4)),
            dma((2, 2)),
        ],
        compiler_params=pltpu.CompilerParams(collective_id=0, has_side_effects=True),
    )(
        device_request,
        batch_blocks,
        batch_atom,
        stored_density_blocks,
        basis_values,
        point_offset,
        point_weight,
        exchange_kernel,
        atom_xyz,
    )

    return pl.pallas_call(
        functools.partial(finish_kernel, batches),
        out_shape=(
            jax.ShapeDtypeStruct((own, tile, tile), BF16),
            jax.ShapeDtypeStruct((batches, points), F32),
            jax.ShapeDtypeStruct((4, atoms), F32),
        ),
        in_specs=[VMEM, VMEM, VMEM],
        out_specs=(VMEM, VMEM, VMEM),
    )(hamiltonian, density, table)


def solution(mesh):
    return jax.shard_map(
        functools.partial(on_device, mesh.shape["grp"], mesh.shape["dev"]),
        mesh=mesh,
        in_specs=(
            P(("grp", "dev"), None, None),
            P("dev", None, None),
            P(("grp", "dev"), None, None),
            P(("grp", "dev"), None),
            P(("grp", "dev")),
            P(None, ("grp", "dev"), None),
            P(("grp", "dev"), None),
            P(("grp", "dev"), None),
            P(),
        ),
        out_specs=(P("dev", None, None), P(("grp", "dev"), None), P()),
        check_vma=False,
    )
```

time: 66.7 us -> 58.8 us (0.88)
  Pallas kernels: 64.2 us -> 56.1 us
    pallas_call x3 -> x2, Pallas kernels: 64.2 us -> 56.1 us  [the longest x1 53.6 us: on_device(): pl.pallas_call(functools.partial(whole_kernel, groups, devs), out_shape=(...]
    unnamed x1 -> x6, local copies, waits for them, and re-layouts: 1.67 us -> 1.87 us
where the time goes in v1:
time: 58.8 us; the launch traced here: 58.6 us
  Pallas kernels  56.1 us (95%)
  local copies, waits for them, and re-layouts  1.87 us (3%)
  between operations  0.65 us (1%)
    pallas_call x1, Pallas kernels, on_device(): pl.pallas_call(functools.partial(whole_kernel, groups, devs), out_shape=(...  53.6 us
    pallas_call x1, Pallas kernels, on_device(): pl.pallas_call(functools.partial(finish_kernel, batches), out_shape=(jax....  2.49 us
    unnamed x6, local copies, waits for them, and re-layouts  1.87 us

profile of v1, /device:TPU:0, one launch (start us, length us, event | category | flops | bytes accessed | tf_op | source)
XLA Modules:
  0.0 58.6 jit_solution(1833247698362792718)
XLA Ops:
  0.6 53.6 %shard_map.112 = (bf16[8,128,128]{2,1,0:T(8,128)(2,1)S(1)}, f32[4,256]{1,0:T(4,128)S(1)}, f32[32,1,128]{2,1,0:T(1,128)S(1)}) custom-call(s32[1,8,8]{2,1,0:T(8,128)} %request.1, s32[4,16]{1,0:T(4,128)} %blocks.1, s32[4]{0:T(128)} %batch_atom.1, bf16[8,128,128]{2,1,0:T(8,128)(2,1)} %stored_any.1, bf16[4,256,512]{2,1,0:T(8,128)(2,1)} %values_any.1, ...), custom_call_target="tpu_custom_call" | custom-call | tf_op jit(solution)/shard_map/pallas_call | solution.py:474
  54.3 0.0 copy-start
  54.3 0.7 %copy-done = bf16[8,128,128]{2,1,0:T(8,128)(2,1)} copy-done((bf16[8,128,128]{2,1,0:T(8,128)(2,1)}, bf16[8,128,128]{2,1,0:T(8,128)(2,1)S(1)}, u32[]{:S(2)}) %copy-start) | copy-done | bytes 262168
  54.9 0.0 copy-start.1
  54.9 0.6 %copy-done.1 = f32[32,1,128]{2,1,0:T(1,128)} copy-done((f32[32,1,128]{2,1,0:T(1,128)}, f32[32,1,128]{2,1,0:T(1,128)S(1)}, u32[]{:S(2)}) %copy-start.1) | copy-done | bytes 16408
  55.5 0.0 copy-start.2
  55.5 0.6 %copy-done.2 = f32[4,256]{1,0:T(4,128)} copy-done((f32[4,256]{1,0:T(4,128)}, f32[4,256]{1,0:T(4,128)S(1)}, u32[]{:S(2)}) %copy-start.2) | copy-done | bytes 4120
  56.1 2.5 %shard_map.113 = (bf16[8,128,128]{2,1,0:T(8,128)(2,1)}, f32[4,256]{1,0:T(4,128)}, f32[4,1000]{1,0:T(4,128)}) custom-call(bf16[8,128,128]{2,1,0:T(8,128)(2,1)} %copy-done, f32[4,256]{1,0:T(4,128)} %copy-done.2, f32[32,1,128]{2,1,0:T(1,128)} %copy-done.1), custom_call_target="tpu_custom_call" | custom-call | tf_op jit(solution)/shard_map/pallas_call | solution.py:523
Async XLA Ops:
  54.3 0.7 %copy-start = (bf16[8,128,128]{2,1,0:T(8,128)(2,1)}, bf16[8,128,128]{2,1,0:T(8,128)(2,1)S(1)}, u32[]{:S(2)}) copy-start(bf16[8,128,128]{2,1,0:T(8,128)(2,1)S(1)} %get-tuple-element.6.hamiltonian) | copy-start | bytes 786436
  54.9 0.6 %copy-start.1 = (f32[32,1,128]{2,1,0:T(1,128)}, f32[32,1,128]{2,1,0:T(1,128)S(1)}, u32[]{:S(2)}) copy-start(f32[32,1,128]{2,1,0:T(1,128)S(1)} %get-tuple-element.8.table) | copy-start | bytes 49156
  55.5 0.6 %copy-start.2 = (f32[4,256]{1,0:T(4,128)}, f32[4,256]{1,0:T(4,128)S(1)}, u32[]{:S(2)}) copy-start(f32[4,256]{1,0:T(4,128)S(1)} %get-tuple-element.7.density) | copy-start | bytes 12292
